TPU v7x, 128 devices: a whole 4x4x4 slice. The times are simulated.
128 devices in a mesh: tm: 32 (over y_hi, z, x), chan: 4 (over y_lo, core).
Axes of the slice: x: 4, y: 4 (y_hi: 2, y_lo: 2; y = y_hi * 2 + y_lo), z: 4, core: 2. Of those that a mesh axis runs over, the one named last changes fastest.
Arguments:
- fwd_in: bfloat16 [65536, 512], P('tm', 'chan'), may hold values from -28 to 28, as said below
- bwd_in: bfloat16 [65536, 512], P('tm', 'chan'), may hold values from -28 to 28, as said below
Outputs:
- forward_error: bfloat16 [65536, 512], P('tm', 'chan')
- backward_error: bfloat16 [65536, 512], P('tm', 'chan')
Inputs may be any that keep to these rules, and one draw needn't show every extreme that they name: `fwd_in`: real-valued samples. `bwd_in`: real-valued samples.
All inputs are finite; a program needn't handle non-finite values.
Results may differ from a plain program's by a relative error of at most 0.0066.
Values may be sent and summed in bfloat16 or wider, within the bound.
A program may use at most 64 MiB of HBM per device.

v0:
```python
import jax
import jax.numpy as jnp
from jax import lax
from jax.sharding import PartitionSpec as P

ORDERS = 2
NSTEPS = 6


HIGH = lax.Precision.HIGHEST


def from_behind(value, axis, by):
    devices = lax.axis_size(axis)
    pairs = [(i, i + by) for i in range(devices) if 0 <= i + by < devices]
    return lax.ppermute(value, axis, pairs)


def gram(left, right):
    return lax.dot_general(
        left, right, (((0,), (0,)), ((), ())), preferred_element_type=jnp.float32
    )


def full_inverse(matrix):
    factor = lax.rsqrt(jnp.sum(matrix * matrix) + 1e-06)
    iterate = factor * jnp.eye(matrix.shape[0], dtype=jnp.float32)
    for step in range(NSTEPS):
        product = jnp.dot(matrix, iterate, precision=HIGH)
        iterate = 2.0 * iterate - jnp.dot(product, iterate, precision=HIGH)
    return iterate


def local(fwd_in, bwd_in):
    arrived = (
        lax.all_to_all(fwd_in, "chan", split_axis=0, concat_axis=1, tiled=True),
        lax.all_to_all(bwd_in, "chan", split_axis=0, concat_axis=1, tiled=True),
    )
    forward = arrived[0]
    backward = arrived[1]
    for order in range(ORDERS):
        before = from_behind(backward[-1:], ("tm", "chan"), 1)
        shifted = jnp.concatenate([before, backward[:-1]], axis=0)
        cov_fwd = gram(forward, forward)
        cov_bwd = gram(shifted, shifted)
        cov_cross = gram(forward, shifted)
        cov_fwd, cov_bwd, cov_cross = lax.psum((cov_fwd, cov_bwd, cov_cross), ("tm", "chan"))
        inv_fwd = full_inverse(cov_fwd)
        inv_bwd = full_inverse(cov_bwd)
        refl_fwd = (-jnp.dot(cov_cross, inv_bwd, precision=HIGH)).astype(jnp.bfloat16)
        refl_bwd = (
            -lax.dot_general(cov_cross, inv_fwd, (((0,), (0,)), ((), ())), precision=HIGH)
        ).astype(jnp.bfloat16)
        new_forward = forward.astype(jnp.float32) + lax.dot_general(
            shifted, refl_fwd, (((1,), (1,)), ((), ())), preferred_element_type=jnp.float32
        )
        new_backward = shifted.astype(jnp.float32) + lax.dot_general(
            forward, refl_bwd, (((1,), (1,)), ((), ())), preferred_element_type=jnp.float32
        )
        forward = new_forward.astype(jnp.bfloat16)
        backward = new_backward.astype(jnp.bfloat16)
    result = (
        lax.all_to_all(forward, "chan", split_axis=1, concat_axis=0, tiled=True),
        lax.all_to_all(backward, "chan", split_axis=1, concat_axis=0, tiled=True),
    )
    return (result[0], result[1])


def solution(mesh):
    in_specs = (P("tm", "chan"), P("tm", "chan"))
    out_specs = (P("tm", "chan"), P("tm", "chan"))
    return jax.shard_map(local, mesh=mesh, in_specs=in_specs, out_specs=out_specs, check_vma=False)
```

profile of v0, /device:TPU:1, one launch (start us, length us, event | category | flops | bytes accessed | tf_op | source)
XLA Modules:
  0.0 490.9 jit_solution(7266842095584646510)
XLA Ops:
  7.2 5.0 %all-to-all-start.1 = ((bf16[4,512,128]{2,1,0:T(8,128)(2,1)}), bf16[4,512,128]{2,1,0:T(8,128)(2,1)S(1)}, u32[]{:S(2)}, u32[]{:S(2)}) async-start(bf16[4,512,128]{2,1,0:T(8,128)(2,1)} %bitcast.154), calls=%async_computation.1 | async-start | bytes 1048576 | tf_op jit(solution)/shard_map/all_to_all | solution.py:37
  13.1 6.8 %all-to-all-done.1 = bf16[4,512,128]{2,1,0:T(8,128)(2,1)S(1)} async-done(((bf16[4,512,128]{2,1,0:T(8,128)(2,1)}), bf16[4,512,128]{2,1,0:T(8,128)(2,1)S(1)}, u32[]{:S(2)}, u32[]{:S(2)}) %all-to-all-start.1) | async-done | bytes 524320 | tf_op jit(solution)/shard_map/all_to_all | solution.py:37
  20.0 4.4 all-to-all-start
  24.4 3.5 collective-permute-start
  28.0 4.3 all-to-all-done
  37.6 156.9 %all-reduce.7.cloned.1.call-done = (f32[512,512]{0,1:T(8,128)}, f32[512,512]{1,0:T(8,128)}, f32[512,512]{1,0:T(8,128)}) async-done(((f32[512,512]{0,1:T(8,128)}, f32[512,512]{1,0:T(8,128)}, f32[512,512]{1,0:T(8,128)}), (f32[512,512]{0,1:T(8,128)}, f32[512,512]{1,0:T(8,128)}, f32[512,512]{1,0:T(8,128)})) %all-reduce.7.cloned.1.call-update) | async-done | bytes 3145744 | tf_op jit(solution)/shard_map/psum | solution.py:47
  194.5 2.5 multiply_reduce_fusion.2
  201.3 1.8 fusion.62
  203.2 1.8 convolution_subtract_fusion.19
  206.9 1.8 convolution_subtract_fusion.18
  208.7 2.1 fusion.64
  210.8 1.8 convolution_subtract_fusion.17
  212.7 1.8 fusion.65
  214.5 1.8 convolution_subtract_fusion.16
  218.3 1.9 convolution_subtract_fusion.15
  222.6 2.2 fusion.19
  224.8 1.8 fusion.68
  226.7 1.8 convolution_subtract_fusion.14
  230.4 1.8 convolution_subtract_fusion.13
  234.1 1.8 convolution_subtract_fusion.12
  236.0 2.0 fusion.71
  238.0 1.8 convolution_subtract_fusion.11
  241.7 1.9 convolution_subtract_fusion.10
  243.6 1.9 fusion.28
  245.4 1.8 fusion.30
  247.8 4.4 collective-permute-start.1
  257.2 153.7 %all-reduce.5.cloned.1.call-done = (f32[512,512]{1,0:T(8,128)}, f32[512,512]{1,0:T(8,128)}, f32[512,512]{1,0:T(8,128)}) async-done(((f32[512,512]{1,0:T(8,128)}, f32[512,512]{1,0:T(8,128)}, f32[512,512]{1,0:T(8,128)}), (f32[512,512]{1,0:T(8,128)}, f32[512,512]{1,0:T(8,128)}, f32[512,512]{1,0:T(8,128)})) %all-reduce.5.cloned.1.call-update) | async-done | bytes 3145744 | tf_op jit(solution)/shard_map/psum | solution.py:47
  410.9 2.2 multiply_reduce_fusion.1
  419.2 1.8 convolution_subtract_fusion.9
  421.0 1.8 fusion.74
  422.9 2.3 convolution_subtract_fusion.8
  425.2 1.8 fusion.75
  427.1 1.8 convolution_subtract_fusion.7
  430.8 1.8 convolution_subtract_fusion.6
  434.5 1.9 convolution_subtract_fusion.5
  436.4 2.0 fusion.31
  439.7 4.8 all-to-all-start.2
  451.5 1.8 convolution_subtract_fusion.4
  453.3 1.8 fusion.80
  455.2 1.8 convolution_subtract_fusion.3
  457.0 2.1 fusion.81
  459.1 1.8 convolution_subtract_fusion.2
  461.0 1.8 fusion.82
  462.8 1.8 convolution_subtract_fusion.1
  466.5 1.8 convolution_subtract_fusion
  468.4 1.9 fusion.33
  471.7 3.5 all-to-all-start.3
  476.2 6.9 %all-to-all-done.3 = bf16[512,4,128]{2,0,1:T(8,128)(2,1)S(1)} async-done(((bf16[512,4,128]{2,0,1:T(8,128)(2,1)}), bf16[512,4,128]{2,0,1:T(8,128)(2,1)S(1)}, u32[]{:S(2)}, u32[]{:S(2)}) %all-to-all-start.3) | async-done | bytes 524320 | tf_op jit(solution)/shard_map/all_to_all | solution.py:64
  (64 shorter events, 48.1 us)
Async XLA Ops:
  7.2 5.0 %copy-start.9 = (bf16[2048,128]{1,0:T(8,128)(2,1)S(1)}, bf16[2048,128]{1,0:T(8,128)(2,1)}, u32[]{:S(2)}) copy-start(bf16[2048,128]{1,0:T(8,128)(2,1)} %param.2) | copy-start | bytes 1572868
  7.2 12.8 %all-to-all-start.1 = ((bf16[4,512,128]{2,1,0:T(8,128)(2,1)}), bf16[4,512,128]{2,1,0:T(8,128)(2,1)S(1)}, u32[]{:S(2)}, u32[]{:S(2)}) async-start(bf16[4,512,128]{2,1,0:T(8,128)(2,1)} %bitcast.154), calls=%async_computation.1 | async-start | bytes 1048576 | tf_op jit(solution)/shard_map/all_to_all | solution.py:37
  20.0 12.3 %all-to-all-start = ((bf16[4,512,128]{1,2,0:T(8,128)(2,1)}), bf16[4,512,128]{1,2,0:T(8,128)(2,1)S(1)}, u32[]{:S(2)}, u32[]{:S(2)}) async-start(bf16[4,512,128]{1,2,0:T(8,128)(2,1)} %copy.9), calls=%async_computation | async-start | bytes 1048576 | tf_op jit(solution)/shard_map/all_to_all | solution.py:36
  24.4 170.1 %all-reduce.7.cloned.1.call-start = ((), (), s32[]{:S(2)}) async-start(), calls=%async_computation.5 | async-start | bytes 6291456 | tf_op jit(solution)/shard_map/psum | solution.py:47
  24.4 10.0 %collective-permute-start = (bf16[1,512]{1,0:T(2,128)(2,1)S(1)}, bf16[1,512]{1,0:T(2,128)(2,1)S(1)}, u32[]{:S(2)}, u32[]{:S(2)}) collective-permute-start(bf16[1,512]{1,0:T(2,128)(2,1)S(1)} %slice_bitcast_fusion), channel_id=1, source_target_pairs={{0,1},{1,2},{2,3},{3,4},{4,5},{5,6},{6,7},{7,8},{8,9},{9,10},{10,1... | collective-permute-start | bytes 3080 | tf_op jit(solution)/shard_map/ppermute | solution.py:16
  37.4 373.5 %all-reduce.5.cloned.1.call-start = ((), (), s32[]{:S(2)}) async-start(), calls=%async_computation.4 | async-start | bytes 6291456 | tf_op jit(solution)/shard_map/psum | solution.py:47
  194.5 3.2 copy-start.2
  218.3 2.6 copy-start.1
  241.7 1.9 copy-start.5
  247.8 7.9 %copy-start.6 = (bf16[512,512]{1,0:T(8,128)(2,1)}, bf16[512,512]{1,0:T(8,128)(2,1)S(1)}, u32[]{:S(2)}) copy-start(bf16[512,512]{1,0:T(8,128)(2,1)S(1)} %add_convert_fusion.1) | copy-start | bytes 1572868
  247.8 6.4 %collective-permute-start.1 = (bf16[1,512]{1,0:T(2,128)(2,1)S(1)}, bf16[1,512]{1,0:T(2,128)(2,1)S(1)}, u32[]{:S(2)}, u32[]{:S(2)}) collective-permute-start(bf16[1,512]{1,0:T(2,128)(2,1)S(1)} %slice.26), channel_id=1, source_target_pairs={{0,1},{1,2},{2,3},{3,4},{4,5},{5,6},{6,7},{7,8},{8,9},{9,10},{10,1... | collective-permute-start | bytes 3080 | tf_op jit(solution)/shard_map/ppermute | solution.py:16
  410.9 2.9 copy-start.3
  434.5 1.9 copy-start.4
  436.4 2.1 copy-start.7
  439.7 4.8 copy-start
  439.7 31.9 %all-to-all-start.2 = ((bf16[512,4,128]{0,2,1:T(8,128)(2,1)}), bf16[512,4,128]{0,2,1:T(8,128)(2,1)S(1)}, u32[]{:S(2)}, u32[]{:S(2)}) async-start(bf16[512,4,128]{0,2,1:T(8,128)(2,1)} %bitcast.155), calls=%async_computation.2 | async-start | bytes 1048576 | tf_op jit(solution)/shard_map/all_to_all | solution.py:63
  468.4 1.9 copy-start.8
  471.7 11.3 %all-to-all-start.3 = ((bf16[512,4,128]{2,0,1:T(8,128)(2,1)}), bf16[512,4,128]{2,0,1:T(8,128)(2,1)S(1)}, u32[]{:S(2)}, u32[]{:S(2)}) async-start(bf16[512,4,128]{2,0,1:T(8,128)(2,1)} %bitcast.133), calls=%async_computation.3 | async-start | bytes 1048576 | tf_op jit(solution)/shard_map/all_to_all | solution.py:64
Sparse Core Ops, SparseCore 0:
  37.5 156.9 all-reduce.6
  257.3 153.4 all-reduce.4
where the time goes:
time: 494 us; the launch traced here: 491 us
  waiting for transfers between devices  329 us (67%)
  matrix products  109 us (22%)
  starting transfers between devices  25.9 us (5%)
  between operations  17.5 us (4%)
  other arithmetic  5.56 us (1%)
    psum x2, waiting for transfers between devices, local(): lax.psum((cov_fwd, cov_bwd, cov_cross), ('tm', 'chan'))  311 us
    dot_general x24, matrix products, full_inverse(): iterate = 2.0 * iterate - jnp.dot(product, iterate, precision=HIGH)  45 us
    dot_general x24, matrix products, full_inverse(): product = jnp.dot(matrix, iterate, precision=HIGH)  44.7 us
  transfers between devices with their start and end apart: 8, of which 5 were waited for; matrix products, arithmetic and copies ran while one was open for 7% of the time, Pallas kernels for 0%

commit v1 on v0

v1 whole, which is shorter than its diff:
```python
import jax
import jax.numpy as jnp
from jax import lax
from jax.experimental import pallas as pl
from jax.experimental.pallas import tpu as pltpu
from jax.sharding import PartitionSpec as P

ORDERS = 2
NSTEPS = 6
C = 512
W = 128
Q = 512
HALO = 16
BLK = 128
TRI = [(i, j) for i in range(4) for j in range(i, 4)]
ROWS = 18 * BLK
PART = ROWS // 3
CH1 = PART // 4
CH2 = CH1 // 4
HALF = 8 * BLK
MESH = pl.DeviceIdType.MESH
f32 = jnp.float32
bf16 = jnp.bfloat16
WIRE = f32


def dot_tn(a, b):
    return lax.dot_general(a, b, (((0,), (0,)), ((), ())), preferred_element_type=f32)


def dot_nt(a, b):
    return lax.dot_general(a, b, (((1,), (1,)), ((), ())), preferred_element_type=f32)


def dot_nn(a, b):
    return lax.dot_general(a, b, (((1,), (0,)), ((), ())), preferred_element_type=f32)


def kernel(
    fwd, bwd, out_f, out_b,
    fbuf, bbuf, wide, u, s1buf, s2buf, g1buf,
    d_send, d_recv, tot, p1, r1, acc1, p2, r2, acc2, p3, r3, fin, fin2,
    zq, amat, obuf,
    x_ssem, x_rsem, h_ssem, h_rsem, hl_sem, d_ssem, d_rsem, c_ssem, c_rsem, o_ssem, o_rsem,
):
    tm = lax.axis_index("tm")
    ch = lax.axis_index("chan")
    y_hi, zx = lax.div(tm, 16), lax.rem(tm, 16)
    z, x = lax.div(zx, 4), lax.rem(zx, 4)
    y_lo, core = lax.div(ch, 2), lax.rem(ch, 2)
    y = y_hi * 2 + y_lo
    partner = (tm, y_lo * 2 + 1 - core)

    def peer(axis, j):
        if axis == 0:
            return (tm - x + lax.rem(x + j, 4), ch)
        if axis == 1:
            ny = lax.rem(y + j, 4)
            return (lax.div(ny, 2) * 16 + zx, lax.rem(ny, 2) * 2 + core)
        return (y_hi * 16 + lax.rem(z + j, 4) * 4 + x, ch)

    pos = (x, y, z)
    nxt = lax.rem(tm + 1, 32)
    prv = lax.rem(tm + 31, 32)

    barrier = pltpu.get_barrier_semaphore()
    for j in (1, 2, 3):
        pl.semaphore_signal(barrier, inc=1, device_id=(tm, lax.rem(ch + j, 4)), device_id_type=MESH)
        for axis in range(3):
            pl.semaphore_signal(barrier, inc=1, device_id=peer(axis, j), device_id_type=MESH)

    @pl.when(ch == 0)
    def _():
        for k in range(4):
            pl.semaphore_signal(barrier, inc=1, device_id=(prv, k), device_id_type=MESH)

    pl.semaphore_wait(barrier, 13)

    def remote(src, dst, ssem, rsem, dev):
        return pltpu.make_async_remote_copy(
            src_ref=src, dst_ref=dst, send_sem=ssem, recv_sem=rsem, device_id=dev, device_id_type=MESH
        )

    mycols = pl.ds(pl.multiple_of(ch * W, W), W)
    myrows = pl.ds(pl.multiple_of(ch * Q, Q), Q)
    copies = []
    for a, (src, dst) in enumerate(((fwd, fbuf), (bwd, bbuf))):
        for j in (1, 2, 3):
            t = lax.rem(ch + j, 4)
            k = lax.rem(t + 3, 4)
            dev = (jnp.where(t == 0, nxt, tm), t)
            cp = remote(
                src.at[pl.ds(pl.multiple_of(k * Q + Q - HALO, HALO), HALO)],
                dst.at[pl.ds(0, HALO), mycols],
                h_ssem.at[a, j - 1], h_rsem.at[a, j - 1], dev,
            )
            cp.start()
            copies.append(cp)
    for j in (2, 1, 3):
        t = lax.rem(ch + j, 4)
        for a, (src, dst) in enumerate(((fwd, fbuf), (bwd, bbuf))):
            cp = remote(
                src.at[pl.ds(pl.multiple_of(t * Q, Q), Q)],
                dst.at[pl.ds(HALO, Q), mycols],
                x_ssem.at[a, j - 1], x_rsem.at[a, j - 1], (tm, t),
            )
            cp.start()
            copies.append(cp)

    @pl.when(ch == 0)
    def _():
        for a, (src, dst) in enumerate(((fwd, fbuf), (bwd, bbuf))):
            remote(
                src.at[pl.ds(4 * Q - HALO, HALO)], dst.at[pl.ds(0, HALO), mycols],
                h_ssem.at[a, 3], hl_sem.at[a], (nxt, ch),
            ).start()

    for src, dst in ((fwd, fbuf), (bwd, bbuf)):
        dst[pl.ds(HALO, Q), mycols] = src[myrows, :]

    @pl.when(ch != 0)
    def _():
        for src, dst in ((fwd, fbuf), (bwd, bbuf)):
            dst[pl.ds(0, HALO), mycols] = src[pl.ds(pl.multiple_of(ch * Q - HALO, HALO), HALO), :]

    for cp in copies:
        cp.wait()

    @pl.when(ch == 0)
    def _():
        for a, (src, dst) in enumerate(((fwd, fbuf), (bwd, bbuf))):
            remote(
                src.at[pl.ds(4 * Q - HALO, HALO)], dst.at[pl.ds(0, HALO), mycols],
                h_ssem.at[a, 3], hl_sem.at[a], (nxt, ch),
            ).wait()

    @pl.when((ch == 0) & (tm == 0))
    def _():
        zero = jnp.zeros((HALO, C), bf16)
        fbuf[pl.ds(0, HALO), :] = zero
        bbuf[pl.ds(0, HALO), :] = zero

    wide[...] = bbuf[...].astype(f32)
    u[0] = fbuf[pl.ds(HALO, Q), :]
    u[1] = wide[pl.ds(HALO - 1, Q), :].astype(bf16)

    def rest():
        s1buf[...] = u[1]
        s2buf[...] = wide[pl.ds(HALO - 2, Q), :].astype(bf16)
        wide[...] = fbuf[...].astype(f32)
        g1buf[...] = wide[pl.ds(HALO - 1, Q), :].astype(bf16)

    order_axes = ((0, 1, 2), (1, 2, 0), (2, 0, 1))

    for order in range(ORDERS):
        other = 1 - core
        po = dot_tn(u[other], u[other])
        for n, (i, j) in enumerate(TRI):
            d_send[order, pl.ds(n * BLK, BLK), :] = po[i * BLK:(i + 1) * BLK, j * BLK:(j + 1) * BLK].astype(WIRE)
        px = dot_tn(u[0, :, pl.ds(pl.multiple_of(other * 256, 256), 256)], u[1])
        for n in range(8):
            i, j = n // 4, n % 4
            d_send[order, pl.ds((10 + n) * BLK, BLK), :] = px[i * BLK:(i + 1) * BLK, j * BLK:(j + 1) * BLK].astype(WIRE)
        swap = remote(d_send.at[order], d_recv.at[order], d_ssem.at[order, 0], d_rsem.at[order, 0], partner)
        swap.start()
        po = dot_tn(u[core], u[core])
        for n, (i, j) in enumerate(TRI):
            tot[pl.ds(n * BLK, BLK), :] = po[i * BLK:(i + 1) * BLK, j * BLK:(j + 1) * BLK]
        px = dot_tn(u[0, :, pl.ds(pl.multiple_of(core * 256, 256), 256)], u[1])
        for n in range(8):
            i, j = n // 4, n % 4
            tot[pl.ds((10 + n) * BLK, BLK), :] = px[i * BLK:(i + 1) * BLK, j * BLK:(j + 1) * BLK]
        swap.wait()
        both = tot[...] + d_recv[order].astype(f32)
        tot[...] = both
        p1[order] = both.astype(WIRE)

        def sends(stage, part, pairs, axis):
            out = []
            for j in (2, 1, 3):
                src, dst = pairs(j)
                cp = remote(
                    src, dst, c_ssem.at[order, stage, part, j - 1], c_rsem.at[order, stage, part, j - 1], peer(axis, j)
                )
                cp.start()
                out.append(cp)
            return out

        st = {}
        for part, (a, b, c) in enumerate(order_axes):
            def pairs(j, part=part, a=a):
                q = lax.rem(pos[a] + j, 4)
                return (
                    p1.at[order, pl.ds(pl.multiple_of(part * PART + q * CH1, 16), CH1)],
                    r1.at[order, part, j - 1],
                )
            st[0, part] = sends(0, part, pairs, a)
        if order == 0:
            rest()
        for part, (a, b, c) in enumerate(order_axes):
            for cp in st[0, part]:
                cp.wait()
            own = tot[pl.ds(pl.multiple_of(part * PART + pos[a] * CH1, 16), CH1), :]
            total = own + r1[order, part, 0].astype(f32) + r1[order, part, 1].astype(f32) + r1[order, part, 2].astype(f32)
            acc1[part] = total
            p2[order, part] = total.astype(WIRE)

            def pairs(j, part=part, b=b):
                q = lax.rem(pos[b] + j, 4)
                return p2.at[order, part, pl.ds(pl.multiple_of(q * CH2, 16), CH2)], r2.at[order, part, j - 1]
            st[1, part] = sends(1, part, pairs, b)
        for part, (a, b, c) in enumerate(order_axes):
            for cp in st[1, part]:
                cp.wait()
            own = acc1[part, pl.ds(pl.multiple_of(pos[b] * CH2, 16), CH2), :]
            total = own + r2[order, part, 0].astype(f32) + r2[order, part, 1].astype(f32) + r2[order, part, 2].astype(f32)
            p3[order, part] = total.astype(WIRE)

            def pairs(j, part=part):
                return p3.at[order, part], r3.at[order, part, j - 1]
            st[2, part] = sends(2, part, pairs, c)
        for part, (a, b, c) in enumerate(order_axes):
            for cp in st[2, part]:
                cp.wait()
            total = (p3[order, part].astype(f32) + r3[order, part, 1].astype(f32)) + (
                r3[order, part, 0].astype(f32) + r3[order, part, 2].astype(f32)
            )
            at = pl.ds(pl.multiple_of(part * PART + pos[a] * CH1 + pos[b] * CH2, 16), CH2)
            fin[order, at, :] = total.astype(WIRE)

            def pairs(j, at=at):
                return fin.at[order, at], fin.at[order, at]
            st[3, part] = sends(3, part, pairs, b)
        for part, (a, b, c) in enumerate(order_axes):
            for cp in st[3, part]:
                cp.wait()
            at = pl.ds(pl.multiple_of(part * PART + pos[a] * CH1, 16), CH1)

            def pairs(j, at=at):
                return fin.at[order, at], fin.at[order, at]
            st[4, part] = sends(4, part, pairs, a)
        for part in range(3):
            for cp in st[4, part]:
                cp.wait()
        swap = remote(
            fin.at[order, pl.ds(10 * BLK, HALF)], fin2.at[order], d_ssem.at[order, 1], d_rsem.at[order, 1], partner
        )
        swap.start()

        square = jnp.zeros((BLK, BLK), f32)
        for n, (i, j) in enumerate(TRI):
            blk = fin[order, pl.ds(n * BLK, BLK), :].astype(f32)
            square = square + (blk * blk if i == j else 2.0 * (blk * blk))
        scale = lax.rsqrt(jnp.sum(square, keepdims=True) + 1e-06)
        for n, (i, j) in enumerate(TRI):
            blk = fin[order, pl.ds(n * BLK, BLK), :].astype(f32) * scale
            zq[pl.ds(C + i * BLK, BLK), pl.ds(j * BLK, BLK)] = blk
            if i != j:
                zq[pl.ds(C + j * BLK, BLK), pl.ds(i * BLK, BLK)] = blk.T
        swap.wait()

        @pl.when(core == 0)
        def _():
            for n in range(8):
                i, j = n // 4, n % 4
                blk = fin[order, pl.ds((10 + n) * BLK, BLK), :].astype(f32) * (-scale)
                zq[pl.ds(j * BLK, BLK), pl.ds(i * BLK, BLK)] = blk.T
                blk = fin2[order, pl.ds(n * BLK, BLK), :].astype(f32) * (-scale)
                zq[pl.ds(j * BLK, BLK), pl.ds((2 + i) * BLK, BLK)] = blk.T

        @pl.when(core == 1)
        def _():
            for n in range(8):
                i, j = n // 4, n % 4
                blk = fin[order, pl.ds((10 + n) * BLK, BLK), :].astype(f32) * (-scale)
                zq[pl.ds((2 + i) * BLK, BLK), pl.ds(j * BLK, BLK)] = blk
                blk = fin2[order, pl.ds(n * BLK, BLK), :].astype(f32) * (-scale)
                zq[pl.ds(i * BLK, BLK), pl.ds(j * BLK, BLK)] = blk

        def step(k, carry):
            v = zq[...]
            hi = v.astype(bf16)
            lo = (v - hi.astype(f32)).astype(bf16)
            prod = dot_nn(hi, hi[C:]) + (dot_nn(hi, lo[C:]) + dot_nn(lo, hi[C:]))
            zq[...] = 2.0 * v - prod
            return carry

        lax.fori_loop(0, NSTEPS - 1, step, 0)
        v = zq[...]
        hi = v.astype(bf16)
        lo = (v - hi.astype(f32)).astype(bf16)
        prod = dot_nn(hi[:C], hi[C:]) + (dot_nn(hi[:C], lo[C:]) + dot_nn(lo[:C], hi[C:]))
        amat[order, core] = (2.0 * v[:C] - prod).astype(bf16)
        swap = remote(
            amat.at[order, core], amat.at[order, core], d_ssem.at[order, 2], d_rsem.at[order, 2], partner
        )
        swap.start()
        swap.wait()
        if order == 0:
            new_f = u[0].astype(f32) + dot_nt(s1buf[...], amat[order, 1])
            new_b = s2buf[...].astype(f32) + dot_nt(g1buf[...], amat[order, 0])
            u[0] = new_f.astype(bf16)
            u[1] = new_b.astype(bf16)
        else:
            new_f = u[0].astype(f32) + dot_nt(u[1], amat[order, 1])
            new_b = u[1].astype(f32) + dot_nt(u[0], amat[order, 0])
            obuf[0] = new_f.astype(bf16)
            obuf[1] = new_b.astype(bf16)

    copies = []
    for j in (2, 1, 3):
        t = lax.rem(ch + j, 4)
        for a, dst in enumerate((out_f, out_b)):
            cp = remote(
                obuf.at[a, :, pl.ds(pl.multiple_of(t * W, W), W)], dst.at[myrows],
                o_ssem.at[a, j - 1], o_rsem.at[a, j - 1], (tm, t),
            )
            cp.start()
            copies.append(cp)
    for a, dst in enumerate((out_f, out_b)):
        dst[myrows, :] = obuf[a, :, mycols]
    for cp in copies:
        cp.wait()


def local(fwd_in, bwd_in):
    vmem = pl.BlockSpec(memory_space=pltpu.VMEM)
    rows = fwd_in.shape[0]
    dma = pltpu.SemaphoreType.DMA
    return pl.pallas_call(
        kernel,
        out_shape=(jax.ShapeDtypeStruct((rows, W), bf16), jax.ShapeDtypeStruct((rows, W), bf16)),
        in_specs=[vmem, vmem],
        out_specs=(vmem, vmem),
        scratch_shapes=[
            pltpu.VMEM((Q + HALO, C), bf16),
            pltpu.VMEM((Q + HALO, C), bf16),
            pltpu.VMEM((Q + HALO, C), f32),
            pltpu.VMEM((2, Q, C), bf16),
            pltpu.VMEM((Q, C), bf16),
            pltpu.VMEM((Q, C), bf16),
            pltpu.VMEM((Q, C), bf16),
            pltpu.VMEM((ORDERS, ROWS, BLK), WIRE),
            pltpu.VMEM((ORDERS, ROWS, BLK), WIRE),
            pltpu.VMEM((ROWS, BLK), f32),
            pltpu.VMEM((ORDERS, ROWS, BLK), WIRE),
            pltpu.VMEM((ORDERS, 3, 3, CH1, BLK), WIRE),
            pltpu.VMEM((3, CH1, BLK), f32),
            pltpu.VMEM((ORDERS, 3, CH1, BLK), WIRE),
            pltpu.VMEM((ORDERS, 3, 3, CH2, BLK), WIRE),
            pltpu.VMEM((3, CH2, BLK), f32),
            pltpu.VMEM((ORDERS, 3, CH2, BLK), WIRE),
            pltpu.VMEM((ORDERS, 3, 3, CH2, BLK), WIRE),
            pltpu.VMEM((ORDERS, ROWS, BLK), WIRE),
            pltpu.VMEM((ORDERS, HALF, BLK), WIRE),
            pltpu.VMEM((2 * C, C), f32),
            pltpu.VMEM((ORDERS, 2, C, C), bf16),
            pltpu.VMEM((2, Q, C), bf16),
            dma((2, 3)), dma((2, 3)), dma((2, 4)), dma((2, 3)), dma((2,)),
            dma((ORDERS, 3)), dma((ORDERS, 3)),
            dma((ORDERS, 5, 3, 3)), dma((ORDERS, 5, 3, 3)),
            dma((2, 3)), dma((2, 3)),
        ],
        compiler_params=pltpu.CompilerParams(
            collective_id=0, has_side_effects=True, vmem_limit_bytes=48 * 1024 * 1024
        ),
        name="lattice",
    )(fwd_in, bwd_in)


def solution(mesh):
    in_specs = (P("tm", "chan"), P("tm", "chan"))
    out_specs = (P("tm", "chan"), P("tm", "chan"))
    return jax.shard_map(local, mesh=mesh, in_specs=in_specs, out_specs=out_specs, check_vma=False)
```

time: 494 us -> 124 us (0.25)
  waiting for transfers between devices: 329 us -> 0 us
  Pallas kernels: 0 us -> 119 us
  matrix products: 109 us -> 0 us
  starting transfers between devices: 25.9 us -> 0 us
  between operations: 17.5 us -> 0.65 us
  other arithmetic: 5.56 us -> 0 us
    psum x2 -> x0, waiting for transfers between devices: 311 us -> none  [local(): lax.psum((cov_fwd, cov_bwd, cov_cross), ('tm', 'chan'))]
    pallas_call x0 -> x1, Pallas kernels: none -> 119 us  [local(): pl.pallas_call(kernel, out_shape=(jax.ShapeDtypeStruct((rows, W), bf16),...]
    dot_general x62 -> x0, matrix products: 109 us -> none  [the longest x24 45 us: full_inverse(): iterate = 2.0 * iterate - jnp.dot(product, iterate, precision=HIGH)]
    all_to_all x4 -> x0, waiting for transfers between devices: 18 us -> none  [the longest x1 6.85 us: local(): lax.all_to_all(backward, 'chan', split_axis=1, concat_axis=0, tiled=True)]
    all_to_all x4 -> x0, starting transfers between devices: 17.7 us -> none  [the longest x1 4.96 us: local(): lax.all_to_all(bwd_in, 'chan', split_axis=0, concat_axis=1, tiled=True)]
    ppermute x2 -> x0, starting transfers between devices: 7.98 us -> none  [from_behind(): return lax.ppermute(value, axis, pairs)]
    reduce_sum x3 -> x0, other arithmetic: 5.56 us -> none  [full_inverse(): factor = lax.rsqrt(jnp.sum(matrix * matrix) + 1e-06)]
  transfers between devices with their start and end apart: 8 -> 0, of which waited for: 5 -> 0; matrix products, arithmetic and copies ran while one was open for 7% -> 0% of each run, Pallas kernels for 0% -> 0%
where the time goes in v1:
time: 124 us; the launch traced here: 123 us
  Pallas kernels  119 us (96%)
  local copies, waits for them, and re-layouts  3.66 us (3%)
    pallas_call x1, Pallas kernels, local(): pl.pallas_call(kernel, out_shape=(jax.ShapeDtypeStruct((rows, W), bf16),...  119 us
    unnamed x6, local copies, waits for them, and re-layouts  3.66 us

profile of v1, /device:TPU:1, one launch (start us, length us, event | category | flops | bytes accessed | tf_op | source)
XLA Modules:
  0.0 123.4 jit_solution(1198934371976515434)
XLA Ops:
  0.6 0.0 copy-start
  0.6 1.0 copy-done
  1.7 0.0 copy-start.1
  1.7 1.0 copy-done.1
  2.7 119.1 %lattice.1 = (bf16[2048,128]{1,0:T(8,128)(2,1)S(1)}, bf16[2048,128]{1,0:T(8,128)(2,1)S(1)}) custom-call(bf16[2048,128]{1,0:T(8,128)(2,1)S(1)} %copy-done, bf16[2048,128]{1,0:T(8,128)(2,1)S(1)} %copy-done.1), custom_call_target="tpu_custom_call" | custom-call | tf_op jit(solution)/shard_map/lattice/pallas_call | solution.py:330
  121.8 0.8 copy.6
  122.6 0.8 copy.7
Async XLA Ops:
  0.6 1.0 copy-start
  1.7 1.0 copy-start.1

commit v2 on v1

v2 whole, which is shorter than its diff:
```python
import jax
import jax.numpy as jnp
from jax import lax
from jax.experimental import pallas as pl
from jax.experimental.pallas import tpu as pltpu
from jax.sharding import PartitionSpec as P

ORDERS = 2
NSTEPS = 6
C = 512
W = 128
Q = 512
HALO = 16
BLK = 128
TRI = [(i, j) for i in range(4) for j in range(i, 4)]
ROWS = 18 * BLK
PART = ROWS // 3
CH1 = PART // 4
CH2 = CH1 // 4
HALF = 8 * BLK
MESH = pl.DeviceIdType.MESH
f32 = jnp.float32
bf16 = jnp.bfloat16
NEAR = bf16
FIRST = bf16


def dot_tn(a, b):
    return lax.dot_general(a, b, (((0,), (0,)), ((), ())), preferred_element_type=f32)


def dot_nt(a, b):
    return lax.dot_general(a, b, (((1,), (1,)), ((), ())), preferred_element_type=f32)


def dot_nn(a, b):
    return lax.dot_general(a, b, (((1,), (0,)), ((), ())), preferred_element_type=f32)


def kernel(
    fwd, bwd, out_f, out_b,
    ff, bb, hf, hb, wide, u, s1buf, s2buf, g1buf, nf, ns,
    d_send, d_recv, tot, p1, r1, p2, r2, p3, r3, fin, fin2,
    zmat, emat, amat,
    l_sem, x_ssem, x_rsem, h_ssem, h_rsem, hl_sem, g_ssem, g_rsem, f_ssem, f_rsem,
    d_ssem, d_rsem, c_ssem, c_rsem,
):
    tm = lax.axis_index("tm")
    ch = lax.axis_index("chan")
    y_hi, zx = lax.div(tm, 16), lax.rem(tm, 16)
    z, x = lax.div(zx, 4), lax.rem(zx, 4)
    y_lo, core = lax.div(ch, 2), lax.rem(ch, 2)
    y = y_hi * 2 + y_lo
    partner = (tm, y_lo * 2 + 1 - core)

    def peer(axis, j):
        if axis == 0:
            return (tm - x + lax.rem(x + j, 4), ch)
        if axis == 1:
            ny = lax.rem(y + j, 4)
            return (lax.div(ny, 2) * 16 + zx, lax.rem(ny, 2) * 2 + core)
        return (y_hi * 16 + lax.rem(z + j, 4) * 4 + x, ch)

    pos = (x, y, z)
    nxt = lax.rem(tm + 1, 32)
    prv = lax.rem(tm + 31, 32)

    barrier = pltpu.get_barrier_semaphore()
    for j in (1, 2, 3):
        pl.semaphore_signal(barrier, inc=1, device_id=(tm, lax.rem(ch + j, 4)), device_id_type=MESH)
        for axis in range(3):
            pl.semaphore_signal(barrier, inc=1, device_id=peer(axis, j), device_id_type=MESH)
    for k in range(4):
        pl.semaphore_signal(barrier, inc=1, device_id=(prv, k), device_id_type=MESH)

    mycols = pl.ds(pl.multiple_of(ch * W, W), W)
    whole = pl.ds(HALO, 4 * Q)
    loads = []
    for a, (src, dst) in enumerate(((fwd, ff), (bwd, bb))):
        cp = pltpu.make_async_copy(src, dst.at[whole, mycols], l_sem.at[a])
        cp.start()
        loads.append(cp)
    pl.semaphore_wait(barrier, 16)
    for cp in loads:
        cp.wait()

    def remote(src, dst, ssem, rsem, dev):
        return pltpu.make_async_remote_copy(
            src_ref=src, dst_ref=dst, send_sem=ssem, recv_sem=rsem, device_id=dev, device_id_type=MESH
        )

    def quarter(t):
        return pl.ds(pl.multiple_of(HALO + t * Q, HALO), Q)

    arrays = ((ff, hf), (bb, hb))
    far = (1 - y_lo) * 2
    copies, late = [], []
    for a, (buf, ahead) in enumerate(arrays):
        for j in (1, 2, 3):
            t = lax.rem(ch + j, 4)
            k = lax.rem(t + 3, 4)
            copies.append(remote(
                buf.at[pl.ds(pl.multiple_of((k + 1) * Q, HALO), HALO), mycols], ahead.at[:, mycols],
                h_ssem.at[a, j - 1], h_rsem.at[a, j - 1], (jnp.where(t == 0, nxt, tm), t),
            ))
    for k in range(2):
        t = far + lax.rem(core + k, 2)
        for a, (buf, ahead) in enumerate(arrays):
            copies.append(remote(
                buf.at[quarter(t), mycols], buf.at[quarter(t), mycols],
                x_ssem.at[a, k], x_rsem.at[a, k], (tm, t),
            ))
    for a, (buf, ahead) in enumerate(arrays):
        copies.append(remote(
            buf.at[whole, mycols], buf.at[whole, mycols], x_ssem.at[a, 2], x_rsem.at[a, 2], partner
        ))
    for a, (buf, ahead) in enumerate(arrays):
        for t in range(4):
            late.append(remote(
                buf.at[pl.ds(4 * Q, HALO), mycols], buf.at[pl.ds(0, HALO), mycols],
                g_ssem.at[a, t], g_rsem.at[a, lax.rem(ch - t + 4, 4)], (nxt, t),
            ))
    for cp in copies + late:
        cp.start()

    def own_ahead(a):
        buf, ahead = arrays[a]
        return remote(
            buf.at[pl.ds(4 * Q, HALO), mycols], ahead.at[:, mycols], h_ssem.at[a, 3], hl_sem.at[a], (nxt, ch)
        )

    @pl.when(ch == 0)
    def _():
        for a in range(2):
            own_ahead(a).start()

    @pl.when(ch != 0)
    def _():
        for buf, ahead in arrays:
            ahead[:, mycols] = buf[pl.ds(pl.multiple_of(ch * Q, HALO), HALO), mycols]

    for cp in copies:
        cp.wait()

    @pl.when(ch == 0)
    def _():
        for a in range(2):
            own_ahead(a).wait()

    @pl.when((ch == 0) & (tm == 0))
    def _():
        hf[...] = jnp.zeros_like(hf)
        hb[...] = jnp.zeros_like(hb)

    def widen(buf, t, ahead):
        if ahead is None:
            wide[...] = buf[pl.ds(pl.multiple_of(t * Q, HALO), Q + HALO), :].astype(f32)
        else:
            wide[pl.ds(0, HALO), :] = ahead[...].astype(f32)
            wide[pl.ds(HALO, Q), :] = buf[quarter(t), :].astype(f32)

    def behind(by):
        return wide[pl.ds(HALO - by, Q), :]

    widen(bb, ch, hb)
    u[0] = ff[quarter(ch), :]
    u[1] = behind(1).astype(bf16)

    def share_quarter():
        out = []
        cols = pl.ds(pl.multiple_of(far * W, 2 * W), 2 * W)
        for a, (buf, ahead) in enumerate(arrays):
            cp = remote(
                buf.at[quarter(ch), cols], buf.at[quarter(ch), cols], f_ssem.at[a, 0], f_rsem.at[a, 0], partner
            )
            cp.start()
            out.append(cp)
        return out

    def send_half():
        out = []
        rows = pl.ds(pl.multiple_of(HALO + y_lo * 2 * Q, HALO), 2 * Q)
        for a, (buf, ahead) in enumerate(arrays):
            cp = remote(
                buf.at[rows, mycols], buf.at[rows, mycols], f_ssem.at[a, 1], f_rsem.at[a, 1], (tm, far + core)
            )
            cp.start()
            out.append(cp)
        return out

    def share_half():
        out = []
        rows = pl.ds(pl.multiple_of(HALO + far * Q, HALO), 2 * Q)
        cols = pl.ds(pl.multiple_of((far + core) * W, W), W)
        for a, (buf, ahead) in enumerate(arrays):
            cp = remote(
                buf.at[rows, cols], buf.at[rows, cols], f_ssem.at[a, 2], f_rsem.at[a, 2], partner
            )
            cp.start()
            out.append(cp)
        return out

    def rest():
        s1buf[...] = u[1]
        s2buf[...] = behind(2).astype(bf16)
        widen(ff, ch, hf)
        g1buf[...] = behind(1).astype(bf16)
        for cp in late:
            cp.wait()

        @pl.when(tm == 0)
        def _():
            ff[pl.ds(0, HALO), :] = jnp.zeros((HALO, C), bf16)
            bb[pl.ds(0, HALO), :] = jnp.zeros((HALO, C), bf16)

    def advance(t):
        rows = pl.ds(pl.multiple_of(t * Q, Q), Q)
        widen(bb, t, None)
        nf[rows, :] = (ff[quarter(t), :].astype(f32) + dot_nt(behind(1).astype(bf16), amat[0, 1])).astype(bf16)
        keep = behind(2)
        widen(ff, t, None)
        ns[rows, :] = (keep + dot_nt(behind(1).astype(bf16), amat[0, 0])).astype(bf16)

    eye = lax.broadcasted_iota(jnp.int32, (BLK, BLK), 0) == lax.broadcasted_iota(jnp.int32, (BLK, BLK), 1)

    def diagonal(m):
        blocks = [jnp.where(eye, m[i * BLK:(i + 1) * BLK, i * BLK:(i + 1) * BLK], 0.0) for i in range(4)]
        return (
            jnp.concatenate([jnp.sum(b, axis=0, keepdims=True) for b in blocks], axis=1),
            jnp.concatenate([jnp.sum(b, axis=1, keepdims=True) for b in blocks], axis=0),
        )

    order_axes = ((0, 1, 2), (1, 2, 0), (2, 0, 1))

    for order in range(ORDERS):
        other = 1 - core
        po = dot_tn(u[other], u[other])
        for n, (i, j) in enumerate(TRI):
            d_send[order, pl.ds(n * BLK, BLK), :] = po[i * BLK:(i + 1) * BLK, j * BLK:(j + 1) * BLK].astype(NEAR)
        px = dot_tn(u[0, :, pl.ds(pl.multiple_of(other * 256, 256), 256)], u[1])
        for n in range(8):
            i, j = n // 4, n % 4
            d_send[order, pl.ds((10 + n) * BLK, BLK), :] = px[i * BLK:(i + 1) * BLK, j * BLK:(j + 1) * BLK].astype(NEAR)
        swap = remote(d_send.at[order], d_recv.at[order], d_ssem.at[order, 0], d_rsem.at[order, 0], partner)
        swap.start()
        po = dot_tn(u[core], u[core])
        for n, (i, j) in enumerate(TRI):
            tot[pl.ds(n * BLK, BLK), :] = po[i * BLK:(i + 1) * BLK, j * BLK:(j + 1) * BLK]
        px = dot_tn(u[0, :, pl.ds(pl.multiple_of(core * 256, 256), 256)], u[1])
        for n in range(8):
            i, j = n // 4, n % 4
            tot[pl.ds((10 + n) * BLK, BLK), :] = px[i * BLK:(i + 1) * BLK, j * BLK:(j + 1) * BLK]
        swap.wait()
        both = tot[...] + d_recv[order].astype(f32)
        tot[...] = both
        p1[order] = both.astype(FIRST)

        def sends(stage, part, pairs, axis):
            out = []
            for j in (2, 1, 3):
                src, dst = pairs(j)
                cp = remote(
                    src, dst, c_ssem.at[order, stage, part, j - 1], c_rsem.at[order, stage, part, j - 1], peer(axis, j)
                )
                cp.start()
                out.append(cp)
            return out

        st = {}
        for part, (a, b, c) in enumerate(order_axes):
            def pairs(j, part=part, a=a):
                q = lax.rem(pos[a] + j, 4)
                return (
                    p1.at[order, pl.ds(pl.multiple_of(part * PART + q * CH1, 16), CH1)],
                    r1.at[order, part, j - 1],
                )
            st[0, part] = sends(0, part, pairs, a)
        if order == 0:
            shares = share_quarter()
            rest()
        else:
            for cp in shares:
                cp.wait()
            shares = share_half()
            rows = pl.ds(pl.multiple_of(ch * Q, Q), Q)
            nf[rows, :] = u[0]
            ns[rows, :] = u[1]
            for cp in shares:
                cp.wait()
            advance(lax.rem(ch + 1, 4))
        for part, (a, b, c) in enumerate(order_axes):
            for cp in st[0, part]:
                cp.wait()
            own = tot[pl.ds(pl.multiple_of(part * PART + pos[a] * CH1, 16), CH1), :]
            total = own + r1[order, part, 0].astype(f32) + r1[order, part, 1].astype(f32) + r1[order, part, 2].astype(f32)
            p2[order, part] = total

            def pairs(j, part=part, b=b):
                q = lax.rem(pos[b] + j, 4)
                return p2.at[order, part, pl.ds(pl.multiple_of(q * CH2, 16), CH2)], r2.at[order, part, j - 1]
            st[1, part] = sends(1, part, pairs, b)
        if order == 1:
            advance(lax.rem(ch + 2, 4))
        for part, (a, b, c) in enumerate(order_axes):
            for cp in st[1, part]:
                cp.wait()
            own = p2[order, part, pl.ds(pl.multiple_of(pos[b] * CH2, 16), CH2), :]
            total = own + r2[order, part, 0] + r2[order, part, 1] + r2[order, part, 2]
            p3[order, part] = total

            def pairs(j, part=part):
                return p3.at[order, part], r3.at[order, part, j - 1]
            st[2, part] = sends(2, part, pairs, c)
        if order == 1:
            advance(lax.rem(ch + 3, 4))
        for part, (a, b, c) in enumerate(order_axes):
            for cp in st[2, part]:
                cp.wait()
            total = (p3[order, part] + r3[order, part, 1]) + (r3[order, part, 0] + r3[order, part, 2])
            at = pl.ds(pl.multiple_of(part * PART + pos[a] * CH1 + pos[b] * CH2, 16), CH2)
            fin[order, at, :] = total

            def pairs(j, at=at):
                return fin.at[order, at], fin.at[order, at]
            st[3, part] = sends(3, part, pairs, b)
        for part, (a, b, c) in enumerate(order_axes):
            for cp in st[3, part]:
                cp.wait()
            at = pl.ds(pl.multiple_of(part * PART + pos[a] * CH1, 16), CH1)

            def pairs(j, at=at):
                return fin.at[order, at], fin.at[order, at]
            st[4, part] = sends(4, part, pairs, a)
        for part in range(3):
            for cp in st[4, part]:
                cp.wait()
        if order == 0:
            for cp in shares:
                cp.wait()
            shares = send_half()
        swap = remote(
            fin.at[order, pl.ds(10 * BLK, HALF)], fin2.at[order], d_ssem.at[order, 1], d_rsem.at[order, 1], partner
        )
        swap.start()

        square = jnp.zeros((BLK, BLK), f32)
        for n, (i, j) in enumerate(TRI):
            blk = fin[order, pl.ds(n * BLK, BLK), :]
            square = square + (blk * blk if i == j else 2.0 * (blk * blk))
        scale = lax.rsqrt(jnp.sum(square, keepdims=True) + 1e-06)
        rows_d, cols_d = [], []
        for n, (i, j) in enumerate(TRI):
            blk = fin[order, pl.ds(n * BLK, BLK), :] * scale
            if i == j:
                only = jnp.where(eye, blk, 0.0)
                rows_d.append(jnp.sum(only, axis=0, keepdims=True))
                cols_d.append(jnp.sum(only, axis=1, keepdims=True))
                emat[pl.ds(i * BLK, BLK), pl.ds(j * BLK, BLK)] = jnp.where(eye, 0.0, blk)
            else:
                emat[pl.ds(i * BLK, BLK), pl.ds(j * BLK, BLK)] = blk
                emat[pl.ds(j * BLK, BLK), pl.ds(i * BLK, BLK)] = blk.T
        swap.wait()

        @pl.when(core == 0)
        def _():
            for n in range(8):
                i, j = n // 4, n % 4
                blk = fin[order, pl.ds((10 + n) * BLK, BLK), :] * (-scale)
                zmat[pl.ds(j * BLK, BLK), pl.ds(i * BLK, BLK)] = blk.T
                blk = fin2[order, pl.ds(n * BLK, BLK), :] * (-scale)
                zmat[pl.ds(j * BLK, BLK), pl.ds((2 + i) * BLK, BLK)] = blk.T

        @pl.when(core == 1)
        def _():
            for n in range(8):
                i, j = n // 4, n % 4
                blk = fin[order, pl.ds((10 + n) * BLK, BLK), :] * (-scale)
                zmat[pl.ds((2 + i) * BLK, BLK), pl.ds(j * BLK, BLK)] = blk
                blk = fin2[order, pl.ds(n * BLK, BLK), :] * (-scale)
                zmat[pl.ds(i * BLK, BLK), pl.ds(j * BLK, BLK)] = blk

        zrows = pl.ds(0, C) if order == 0 else pl.ds(pl.multiple_of(y_lo * 2 * W, 2 * W), 2 * W)

        def step(k, carry):
            dr, dc = carry
            e = emat[...]
            eb = e.astype(bf16)
            te = dot_nn(eb, eb)
            tr, tc = diagonal(te)
            zv = zmat[zrows, :]
            zmat[zrows, :] = zv * (2.0 - dr) - dot_nn(zv.astype(bf16), eb)
            emat[...] = e * ((2.0 - dc) - dr) - te
            for i in range(4):
                at = pl.ds(i * BLK, BLK)
                emat[at, at] = jnp.where(eye, 0.0, emat[at, at])
            return 2.0 * dr - dr * dr - tr, 2.0 * dc - dc * dc - tc

        dr, dc = lax.fori_loop(
            0, NSTEPS - 1, step, (jnp.concatenate(rows_d, axis=1), jnp.concatenate(cols_d, axis=0))
        )
        zv = zmat[zrows, :]
        amat[order, core, zrows, :] = (
            zv * (2.0 - dr) - dot_nn(zv.astype(bf16), emat[...].astype(bf16))
        ).astype(bf16)
        if order == 0:
            part_rows = pl.ds(0, C)
        else:
            part_rows = pl.ds(pl.multiple_of((y_lo * 2 + 1 - core) * W, W), W)
        swap = remote(
            amat.at[order, core, part_rows], amat.at[order, core, part_rows],
            d_ssem.at[order, 2], d_rsem.at[order, 2], partner,
        )
        swap.start()
        swap.wait()
        if order == 0:
            new_f = u[0].astype(f32) + dot_nt(s1buf[...], amat[order, 1])
            new_b = s2buf[...].astype(f32) + dot_nt(g1buf[...], amat[order, 0])
            u[0] = new_f.astype(bf16)
            u[1] = new_b.astype(bf16)

    for t in range(4):
        rows = pl.ds(t * Q, Q)
        out_f[rows, :] = (nf[rows, mycols].astype(f32) + dot_nt(ns[rows, :], amat[1, 1, mycols, :])).astype(bf16)
        out_b[rows, :] = (ns[rows, mycols].astype(f32) + dot_nt(nf[rows, :], amat[1, 0, mycols, :])).astype(bf16)


def local(fwd_in, bwd_in):
    vmem = pl.BlockSpec(memory_space=pltpu.VMEM)
    hbm = pl.BlockSpec(memory_space=pltpu.HBM)
    rows = fwd_in.shape[0]
    dma = pltpu.SemaphoreType.DMA
    return pl.pallas_call(
        kernel,
        out_shape=(jax.ShapeDtypeStruct((rows, W), bf16), jax.ShapeDtypeStruct((rows, W), bf16)),
        in_specs=[hbm, hbm],
        out_specs=(vmem, vmem),
        scratch_shapes=[
            pltpu.VMEM((HALO + rows, C), bf16),
            pltpu.VMEM((HALO + rows, C), bf16),
            pltpu.VMEM((HALO, C), bf16),
            pltpu.VMEM((HALO, C), bf16),
            pltpu.VMEM((Q + HALO, C), f32),
            pltpu.VMEM((2, Q, C), bf16),
            pltpu.VMEM((Q, C), bf16),
            pltpu.VMEM((Q, C), bf16),
            pltpu.VMEM((Q, C), bf16),
            pltpu.VMEM((rows, C), bf16),
            pltpu.VMEM((rows, C), bf16),
            pltpu.VMEM((ORDERS, ROWS, BLK), NEAR),
            pltpu.VMEM((ORDERS, ROWS, BLK), NEAR),
            pltpu.VMEM((ROWS, BLK), f32),
            pltpu.VMEM((ORDERS, ROWS, BLK), FIRST),
            pltpu.VMEM((ORDERS, 3, 3, CH1, BLK), FIRST),
            pltpu.VMEM((ORDERS, 3, CH1, BLK), f32),
            pltpu.VMEM((ORDERS, 3, 3, CH2, BLK), f32),
            pltpu.VMEM((ORDERS, 3, CH2, BLK), f32),
            pltpu.VMEM((ORDERS, 3, 3, CH2, BLK), f32),
            pltpu.VMEM((ORDERS, ROWS, BLK), f32),
            pltpu.VMEM((ORDERS, HALF, BLK), f32),
            pltpu.VMEM((C, C), f32),
            pltpu.VMEM((C, C), f32),
            pltpu.VMEM((ORDERS, 2, C, C), bf16),
            dma((2,)), dma((2, 3)), dma((2, 3)), dma((2, 4)), dma((2, 3)), dma((2,)),
            dma((2, 4)), dma((2, 4)), dma((2, 3)), dma((2, 3)),
            dma((ORDERS, 3)), dma((ORDERS, 3)),
            dma((ORDERS, 5, 3, 3)), dma((ORDERS, 5, 3, 3)),
        ],
        compiler_params=pltpu.CompilerParams(
            collective_id=0, has_side_effects=True, vmem_limit_bytes=56 * 1024 * 1024
        ),
        name="lattice",
    )(fwd_in, bwd_in)


def solution(mesh):
    in_specs = (P("tm", "chan"), P("tm", "chan"))
    out_specs = (P("tm", "chan"), P("tm", "chan"))
    return jax.shard_map(local, mesh=mesh, in_specs=in_specs, out_specs=out_specs, check_vma=False)
```

time: 124 us -> 95.5 us (0.77)
  Pallas kernels: 119 us -> 92 us
    pallas_call x1, Pallas kernels: 119 us -> 92 us  [local(): pl.pallas_call(kernel, out_shape=(jax.ShapeDtypeStruct((rows, W), bf16),...]
    unnamed x6 -> x4, local copies, waits for them, and re-layouts: 3.66 us -> 2.72 us
where the time goes in v2:
time: 95.5 us; the launch traced here: 95.4 us
  Pallas kernels  92 us (96%)
  local copies, waits for them, and re-layouts  2.72 us (3%)
    pallas_call x1, Pallas kernels, local(): pl.pallas_call(kernel, out_shape=(jax.ShapeDtypeStruct((rows, W), bf16),...  92 us
    unnamed x4, local copies, waits for them, and re-layouts  2.72 us

profile of v2, /device:TPU:1, one launch (start us, length us, event | category | flops | bytes accessed | tf_op | source)
XLA Modules:
  0.0 95.4 jit_solution(15517398776688688264)
XLA Ops:
  0.6 92.0 %lattice.1 = (bf16[2048,128]{1,0:T(8,128)(2,1)}, bf16[2048,128]{1,0:T(8,128)(2,1)}) custom-call(bf16[2048,128]{1,0:T(8,128)(2,1)} %fwd.1, bf16[2048,128]{1,0:T(8,128)(2,1)} %bwd.1), custom_call_target="tpu_custom_call" | custom-call | tf_op jit(solution)/shard_map/lattice/pallas_call | solution.py:432
  92.7 0.0 copy-start
  92.7 1.9 %copy.6 = bf16[2048,128]{1,0:T(8,128)(2,1)} copy(bf16[2048,128]{1,0:T(8,128)(2,1)} %get-tuple-element.4) | data formatting | bytes 1048576
  94.6 0.0 copy-done
  94.6 0.8 copy.7
Async XLA Ops:
  92.7 1.9 %copy-start = (bf16[2048,128]{1,0:T(8,128)(2,1)S(1)}, bf16[2048,128]{1,0:T(8,128)(2,1)}, u32[]{:S(2)}) copy-start(bf16[2048,128]{1,0:T(8,128)(2,1)} %get-tuple-element.5) | copy-start | bytes 1572868

commit v3 on v2

--- a/solution.py
+++ b/solution.py
@@ -13,10 +13,8 @@
 HALO = 16
 BLK = 128
 TRI = [(i, j) for i in range(4) for j in range(i, 4)]
-ROWS = 18 * BLK
-PART = ROWS // 3
-CH1 = PART // 4
-CH2 = CH1 // 4
+GROUPS = ((0, 1536, 512, 128, 32), (1536, 1152, 384, 96, 24))
+ROWS = 2688
 HALF = 8 * BLK
 MESH = pl.DeviceIdType.MESH
 f32 = jnp.float32
@@ -40,11 +38,12 @@
 def kernel(
     fwd, bwd, out_f, out_b,
     ff, bb, hf, hb, wide, u, s1buf, s2buf, g1buf, nf, ns,
-    d_send, d_recv, tot, p1, r1, p2, r2, p3, r3, fin, fin2,
-    zmat, emat, amat,
+    d_send, d_recv, tot, p1, r1a, r1b, p2a, p2b, r2a, r2b, p3a, p3b, r3a, r3b, fin_a, fin_b, far_half,
+    zmat, emat, xmat, amat,
     l_sem, x_ssem, x_rsem, h_ssem, h_rsem, hl_sem, g_ssem, g_rsem, f_ssem, f_rsem,
     d_ssem, d_rsem, c_ssem, c_rsem,
 ):
+    r1, p2, r2, p3, r3, fin = (r1a, r1b), (p2a, p2b), (r2a, r2b), (p3a, p3b), (r3a, r3b), (fin_a, fin_b)
     tm = lax.axis_index("tm")
     ch = lax.axis_index("chan")
     y_hi, zx = lax.div(tm, 16), lax.rem(tm, 16)
@@ -231,50 +230,135 @@
         )
 
     order_axes = ((0, 1, 2), (1, 2, 0), (2, 0, 1))
-
-    for order in range(ORDERS):
-        other = 1 - core
-        po = dot_tn(u[other], u[other])
+    other = 1 - core
+
+    def half(k):
+        return u[0, :, pl.ds(pl.multiple_of(k * 256, 256), 256)]
+
+    def put_tri(dst, m):
         for n, (i, j) in enumerate(TRI):
-            d_send[order, pl.ds(n * BLK, BLK), :] = po[i * BLK:(i + 1) * BLK, j * BLK:(j + 1) * BLK].astype(NEAR)
-        px = dot_tn(u[0, :, pl.ds(pl.multiple_of(other * 256, 256), 256)], u[1])
+            dst[pl.ds(n * BLK, BLK), :] = m[i * BLK:(i + 1) * BLK, j * BLK:(j + 1) * BLK].astype(dst.dtype)
+
+    def put_cross(dst, m):
         for n in range(8):
             i, j = n // 4, n % 4
-            d_send[order, pl.ds((10 + n) * BLK, BLK), :] = px[i * BLK:(i + 1) * BLK, j * BLK:(j + 1) * BLK].astype(NEAR)
-        swap = remote(d_send.at[order], d_recv.at[order], d_ssem.at[order, 0], d_rsem.at[order, 0], partner)
-        swap.start()
-        po = dot_tn(u[core], u[core])
-        for n, (i, j) in enumerate(TRI):
-            tot[pl.ds(n * BLK, BLK), :] = po[i * BLK:(i + 1) * BLK, j * BLK:(j + 1) * BLK]
-        px = dot_tn(u[0, :, pl.ds(pl.multiple_of(core * 256, 256), 256)], u[1])
-        for n in range(8):
-            i, j = n // 4, n % 4
-            tot[pl.ds((10 + n) * BLK, BLK), :] = px[i * BLK:(i + 1) * BLK, j * BLK:(j + 1) * BLK]
-        swap.wait()
-        both = tot[...] + d_recv[order].astype(f32)
-        tot[...] = both
-        p1[order] = both.astype(FIRST)
-
-        def sends(stage, part, pairs, axis):
+            dst[pl.ds(GROUPS[1][0] + n * BLK, BLK), :] = m[
+                i * BLK:(i + 1) * BLK, j * BLK:(j + 1) * BLK
+            ].astype(dst.dtype)
+
+    lane = lax.broadcasted_iota(jnp.int32, (BLK, BLK), 1)
+    row = lax.broadcasted_iota(jnp.int32, (BLK, BLK), 0)
+    kept = ((lane > row) & ~((row == 0) & (lane == BLK - 1))) | ((row == BLK - 1) & (lane == 0))
+
+    for order in range(ORDERS):
+        swapped = pl.ds(0, 10 * BLK), pl.ds(GROUPS[1][0], HALF)
+
+        def swap_part(k):
+            return remote(
+                d_send.at[order, swapped[k]], d_recv.at[order, swapped[k]],
+                d_ssem.at[order, k], d_rsem.at[order, k], partner,
+            )
+
+        put_tri(d_send.at[order], dot_tn(u[other], u[other]))
+        swap_part(0).start()
+        put_cross(d_send.at[order], dot_tn(half(other), u[1]))
+        swap_part(1).start()
+        put_tri(tot, dot_tn(u[core], u[core]))
+
+        def sends(g, stage, part, pairs, axis):
             out = []
             for j in (2, 1, 3):
                 src, dst = pairs(j)
                 cp = remote(
-                    src, dst, c_ssem.at[order, stage, part, j - 1], c_rsem.at[order, stage, part, j - 1], peer(axis, j)
+                    src, dst, c_ssem.at[order, g, stage, part, j - 1], c_rsem.at[order, g, stage, part, j - 1],
+                    peer(axis, j),
                 )
                 cp.start()
                 out.append(cp)
             return out
 
         st = {}
-        for part, (a, b, c) in enumerate(order_axes):
-            def pairs(j, part=part, a=a):
-                q = lax.rem(pos[a] + j, 4)
-                return (
-                    p1.at[order, pl.ds(pl.multiple_of(part * PART + q * CH1, 16), CH1)],
-                    r1.at[order, part, j - 1],
-                )
-            st[0, part] = sends(0, part, pairs, a)
+
+        def done(g, stage, part):
+            for cp in st[g, stage, part]:
+                cp.wait()
+
+        def stage0(g):
+            base, rows, size, c1, c2 = GROUPS[g]
+            swap_part(g).wait()
+            at = swapped[g]
+            both = tot[at, :] + d_recv[order, at, :].astype(f32)
+            tot[at, :] = both
+            p1[order, at, :] = both.astype(FIRST)
+            for part, (a, b, c) in enumerate(order_axes):
+                def pairs(j):
+                    q = lax.rem(pos[a] + j, 4)
+                    return (
+                        p1.at[order, pl.ds(pl.multiple_of(base + part * size + q * c1, 16), c1)],
+                        r1[g].at[order, part, j - 1],
+                    )
+                st[g, 0, part] = sends(g, 0, part, pairs, a)
+
+        def stage1(g):
+            base, rows, size, c1, c2 = GROUPS[g]
+            for part, (a, b, c) in enumerate(order_axes):
+                done(g, 0, part)
+                r = r1[g]
+                own = tot[pl.ds(pl.multiple_of(base + part * size + pos[a] * c1, 16), c1), :]
+                p2[g][order, part] = own + r[order, part, 0].astype(f32) + r[order, part, 1].astype(f32) + r[
+                    order, part, 2
+                ].astype(f32)
+
+                def pairs(j):
+                    q = lax.rem(pos[b] + j, 4)
+                    return p2[g].at[order, part, pl.ds(pl.multiple_of(q * c2, 8), c2)], r2[g].at[order, part, j - 1]
+                st[g, 1, part] = sends(g, 1, part, pairs, b)
+
+        def stage2(g):
+            base, rows, size, c1, c2 = GROUPS[g]
+            for part, (a, b, c) in enumerate(order_axes):
+                done(g, 1, part)
+                r = r2[g]
+                own = p2[g][order, part, pl.ds(pl.multiple_of(pos[b] * c2, 8), c2), :]
+                p3[g][order, part] = own + r[order, part, 0] + r[order, part, 1] + r[order, part, 2]
+
+                def pairs(j):
+                    return p3[g].at[order, part], r3[g].at[order, part, j - 1]
+                st[g, 2, part] = sends(g, 2, part, pairs, c)
+
+        def stage3(g):
+            base, rows, size, c1, c2 = GROUPS[g]
+            for part, (a, b, c) in enumerate(order_axes):
+                done(g, 2, part)
+                r = r3[g]
+                total = (p3[g][order, part] + r[order, part, 1]) + (r[order, part, 0] + r[order, part, 2])
+                at = pl.ds(pl.multiple_of(part * size + pos[a] * c1 + pos[b] * c2, c2), c2)
+                if g == 0:
+                    n = part * 4 + pos[a]
+                    first = lax.broadcasted_iota(jnp.int32, (c2, BLK), 0) + pos[b] * c2
+                    ahead = lax.broadcasted_iota(jnp.int32, (c2, BLK), 1) == lax.rem(first + BLK - 1, BLK)
+                    on = (n == 0) | (n == 4) | (n == 7) | (n == 9)
+                    low = total - total.astype(bf16).astype(f32)
+                    total = jnp.where(ahead & on, pltpu.roll(low, BLK - 1, 1), total)
+                fin[g][order, at, :] = total.astype(fin[g].dtype)
+
+                def pairs(j):
+                    return fin[g].at[order, at], fin[g].at[order, at]
+                st[g, 3, part] = sends(g, 3, part, pairs, b)
+
+        def stage4(g):
+            base, rows, size, c1, c2 = GROUPS[g]
+            for part, (a, b, c) in enumerate(order_axes):
+                done(g, 3, part)
+                at = pl.ds(pl.multiple_of(part * size + pos[a] * c1, c1), c1)
+
+                def pairs(j):
+                    return fin[g].at[order, at], fin[g].at[order, at]
+                st[g, 4, part] = sends(g, 4, part, pairs, a)
+
+        stage0(0)
+        put_cross(tot, dot_tn(half(core), u[1]))
+        stage0(1)
         if order == 0:
             shares = share_quarter()
             rest()
@@ -287,128 +371,116 @@
             ns[rows, :] = u[1]
             for cp in shares:
                 cp.wait()
+        stage1(0)
+        if order == 1:
             advance(lax.rem(ch + 1, 4))
-        for part, (a, b, c) in enumerate(order_axes):
-            for cp in st[0, part]:
-                cp.wait()
-            own = tot[pl.ds(pl.multiple_of(part * PART + pos[a] * CH1, 16), CH1), :]
-            total = own + r1[order, part, 0].astype(f32) + r1[order, part, 1].astype(f32) + r1[order, part, 2].astype(f32)
-            p2[order, part] = total
-
-            def pairs(j, part=part, b=b):
-                q = lax.rem(pos[b] + j, 4)
-                return p2.at[order, part, pl.ds(pl.multiple_of(q * CH2, 16), CH2)], r2.at[order, part, j - 1]
-            st[1, part] = sends(1, part, pairs, b)
+        stage1(1)
+        stage2(0)
         if order == 1:
             advance(lax.rem(ch + 2, 4))
-        for part, (a, b, c) in enumerate(order_axes):
-            for cp in st[1, part]:
-                cp.wait()
-            own = p2[order, part, pl.ds(pl.multiple_of(pos[b] * CH2, 16), CH2), :]
-            total = own + r2[order, part, 0] + r2[order, part, 1] + r2[order, part, 2]
-            p3[order, part] = total
-
-            def pairs(j, part=part):
-                return p3.at[order, part], r3.at[order, part, j - 1]
-            st[2, part] = sends(2, part, pairs, c)
+        stage2(1)
+        stage3(0)
+        stage3(1)
+        stage4(0)
         if order == 1:
             advance(lax.rem(ch + 3, 4))
-        for part, (a, b, c) in enumerate(order_axes):
-            for cp in st[2, part]:
-                cp.wait()
-            total = (p3[order, part] + r3[order, part, 1]) + (r3[order, part, 0] + r3[order, part, 2])
-            at = pl.ds(pl.multiple_of(part * PART + pos[a] * CH1 + pos[b] * CH2, 16), CH2)
-            fin[order, at, :] = total
-
-            def pairs(j, at=at):
-                return fin.at[order, at], fin.at[order, at]
-            st[3, part] = sends(3, part, pairs, b)
-        for part, (a, b, c) in enumerate(order_axes):
-            for cp in st[3, part]:
-                cp.wait()
-            at = pl.ds(pl.multiple_of(part * PART + pos[a] * CH1, 16), CH1)
-
-            def pairs(j, at=at):
-                return fin.at[order, at], fin.at[order, at]
-            st[4, part] = sends(4, part, pairs, a)
         for part in range(3):
-            for cp in st[4, part]:
-                cp.wait()
+            done(0, 4, part)
+        stage4(1)
         if order == 0:
             for cp in shares:
                 cp.wait()
             shares = send_half()
-        swap = remote(
-            fin.at[order, pl.ds(10 * BLK, HALF)], fin2.at[order], d_ssem.at[order, 1], d_rsem.at[order, 1], partner
-        )
-        swap.start()
 
         square = jnp.zeros((BLK, BLK), f32)
+        whole_d, rows_d, cols_d = [], [], []
         for n, (i, j) in enumerate(TRI):
-            blk = fin[order, pl.ds(n * BLK, BLK), :]
-            square = square + (blk * blk if i == j else 2.0 * (blk * blk))
-        scale = lax.rsqrt(jnp.sum(square, keepdims=True) + 1e-06)
-        rows_d, cols_d = [], []
-        for n, (i, j) in enumerate(TRI):
-            blk = fin[order, pl.ds(n * BLK, BLK), :] * scale
+            blk = fin[0][order, pl.ds(n * BLK, BLK), :].astype(f32)
             if i == j:
-                only = jnp.where(eye, blk, 0.0)
+                only = jnp.where(eye, blk + pltpu.roll(blk, 1, 1), 0.0)
+                upper = jnp.where(kept, blk, 0.0)
+                square = square + (only * only + 2.0 * (upper * upper))
                 rows_d.append(jnp.sum(only, axis=0, keepdims=True))
                 cols_d.append(jnp.sum(only, axis=1, keepdims=True))
-                emat[pl.ds(i * BLK, BLK), pl.ds(j * BLK, BLK)] = jnp.where(eye, 0.0, blk)
+                emat[pl.ds(i * BLK, BLK), pl.ds(j * BLK, BLK)] = upper + upper.T
             else:
+                square = square + 2.0 * (blk * blk)
                 emat[pl.ds(i * BLK, BLK), pl.ds(j * BLK, BLK)] = blk
                 emat[pl.ds(j * BLK, BLK), pl.ds(i * BLK, BLK)] = blk.T
+        scale = lax.rsqrt(jnp.sum(square, keepdims=True) + 1e-06)
+        dr = jnp.concatenate(rows_d, axis=1) * scale
+        dc = jnp.concatenate(cols_d, axis=0) * scale
+
+        def set_diagonal(ref, value):
+            for i in range(4):
+                at = pl.ds(i * BLK, BLK)
+                ref[at, at] = jnp.where(eye, value[:, i * BLK:(i + 1) * BLK], ref[at, at])
+
+        def clear_diagonal(ref):
+            for i in range(4):
+                at = pl.ds(i * BLK, BLK)
+                ref[at, at] = jnp.where(eye, 0.0, ref[at, at])
+
+        e = emat[...] * scale
+        xmat[...] = -e
+        set_diagonal(xmat, 2.0 - dr)
+        for k in range(NSTEPS - 1):
+            eb = e.astype(bf16)
+            if k > 0:
+                xv = xmat[...]
+                xmat[...] = xv * (2.0 - dr) - dot_nn(xv.astype(bf16), eb)
+            te = dot_nn(eb, eb)
+            tr, tc = diagonal(te)
+            emat[...] = e * ((2.0 - dc) - dr) - te
+            clear_diagonal(emat)
+            e = emat[...]
+            dr, dc = 2.0 * dr - dr * dr - tr, 2.0 * dc - dc * dc - tc
+            if k == 2:
+                for part in range(3):
+                    done(1, 4, part)
+                swap = remote(
+                    fin[1].at[order, pl.ds(0, HALF)], far_half.at[order],
+                    d_ssem.at[order, 2], d_rsem.at[order, 2], partner,
+                )
+                swap.start()
+        xv = xmat[...]
+        xmat[...] = xv * (2.0 - dr) - dot_nn(xv.astype(bf16), e.astype(bf16))
         swap.wait()
 
         @pl.when(core == 0)
         def _():
             for n in range(8):
                 i, j = n // 4, n % 4
-                blk = fin[order, pl.ds((10 + n) * BLK, BLK), :] * (-scale)
+                blk = fin[1][order, pl.ds(n * BLK, BLK), :]
                 zmat[pl.ds(j * BLK, BLK), pl.ds(i * BLK, BLK)] = blk.T
-                blk = fin2[order, pl.ds(n * BLK, BLK), :] * (-scale)
+                blk = far_half[order, pl.ds(n * BLK, BLK), :]
                 zmat[pl.ds(j * BLK, BLK), pl.ds((2 + i) * BLK, BLK)] = blk.T
 
         @pl.when(core == 1)
         def _():
             for n in range(8):
                 i, j = n // 4, n % 4
-                blk = fin[order, pl.ds((10 + n) * BLK, BLK), :] * (-scale)
+                blk = fin[1][order, pl.ds(n * BLK, BLK), :]
                 zmat[pl.ds((2 + i) * BLK, BLK), pl.ds(j * BLK, BLK)] = blk
-                blk = fin2[order, pl.ds(n * BLK, BLK), :] * (-scale)
+                blk = far_half[order, pl.ds(n * BLK, BLK), :]
                 zmat[pl.ds(i * BLK, BLK), pl.ds(j * BLK, BLK)] = blk
 
         zrows = pl.ds(0, C) if order == 0 else pl.ds(pl.multiple_of(y_lo * 2 * W, 2 * W), 2 * W)
-
-        def step(k, carry):
-            dr, dc = carry
-            e = emat[...]
-            eb = e.astype(bf16)
-            te = dot_nn(eb, eb)
-            tr, tc = diagonal(te)
-            zv = zmat[zrows, :]
-            zmat[zrows, :] = zv * (2.0 - dr) - dot_nn(zv.astype(bf16), eb)
-            emat[...] = e * ((2.0 - dc) - dr) - te
-            for i in range(4):
-                at = pl.ds(i * BLK, BLK)
-                emat[at, at] = jnp.where(eye, 0.0, emat[at, at])
-            return 2.0 * dr - dr * dr - tr, 2.0 * dc - dc * dc - tc
-
-        dr, dc = lax.fori_loop(
-            0, NSTEPS - 1, step, (jnp.concatenate(rows_d, axis=1), jnp.concatenate(cols_d, axis=0))
-        )
         zv = zmat[zrows, :]
-        amat[order, core, zrows, :] = (
-            zv * (2.0 - dr) - dot_nn(zv.astype(bf16), emat[...].astype(bf16))
-        ).astype(bf16)
+        zh = zv.astype(bf16)
+        zl = (zv - zh.astype(f32)).astype(bf16)
+        xv = xmat[...]
+        xh = xv.astype(bf16)
+        xl = (xv - xh.astype(f32)).astype(bf16)
+        prod = dot_nn(zh, xh) + (dot_nn(zh, xl) + dot_nn(zl, xh))
+        amat[order, core, zrows, :] = (prod * (-scale)).astype(bf16)
         if order == 0:
             part_rows = pl.ds(0, C)
         else:
             part_rows = pl.ds(pl.multiple_of((y_lo * 2 + 1 - core) * W, W), W)
         swap = remote(
             amat.at[order, core, part_rows], amat.at[order, core, part_rows],
-            d_ssem.at[order, 2], d_rsem.at[order, 2], partner,
+            d_ssem.at[order, 3], d_rsem.at[order, 3], partner,
         )
         swap.start()
         swap.wait()
@@ -450,20 +522,27 @@
             pltpu.VMEM((ORDERS, ROWS, BLK), NEAR),
             pltpu.VMEM((ROWS, BLK), f32),
             pltpu.VMEM((ORDERS, ROWS, BLK), FIRST),
-            pltpu.VMEM((ORDERS, 3, 3, CH1, BLK), FIRST),
-            pltpu.VMEM((ORDERS, 3, CH1, BLK), f32),
-            pltpu.VMEM((ORDERS, 3, 3, CH2, BLK), f32),
-            pltpu.VMEM((ORDERS, 3, CH2, BLK), f32),
-            pltpu.VMEM((ORDERS, 3, 3, CH2, BLK), f32),
-            pltpu.VMEM((ORDERS, ROWS, BLK), f32),
+            pltpu.VMEM((ORDERS, 3, 3, 128, BLK), FIRST),
+            pltpu.VMEM((ORDERS, 3, 3, 96, BLK), FIRST),
+            pltpu.VMEM((ORDERS, 3, 128, BLK), f32),
+            pltpu.VMEM((ORDERS, 3, 96, BLK), f32),
+            pltpu.VMEM((ORDERS, 3, 3, 32, BLK), f32),
+            pltpu.VMEM((ORDERS, 3, 3, 24, BLK), f32),
+            pltpu.VMEM((ORDERS, 3, 32, BLK), f32),
+            pltpu.VMEM((ORDERS, 3, 24, BLK), f32),
+            pltpu.VMEM((ORDERS, 3, 3, 32, BLK), f32),
+            pltpu.VMEM((ORDERS, 3, 3, 24, BLK), f32),
+            pltpu.VMEM((ORDERS, 1536, BLK), bf16),
+            pltpu.VMEM((ORDERS, 1152, BLK), f32),
             pltpu.VMEM((ORDERS, HALF, BLK), f32),
+            pltpu.VMEM((C, C), f32),
             pltpu.VMEM((C, C), f32),
             pltpu.VMEM((C, C), f32),
             pltpu.VMEM((ORDERS, 2, C, C), bf16),
             dma((2,)), dma((2, 3)), dma((2, 3)), dma((2, 4)), dma((2, 3)), dma((2,)),
             dma((2, 4)), dma((2, 4)), dma((2, 3)), dma((2, 3)),
-            dma((ORDERS, 3)), dma((ORDERS, 3)),
-            dma((ORDERS, 5, 3, 3)), dma((ORDERS, 5, 3, 3)),
+            dma((ORDERS, 4)), dma((ORDERS, 4)),
+            dma((ORDERS, 2, 5, 3, 3)), dma((ORDERS, 2, 5, 3, 3)),
         ],
         compiler_params=pltpu.CompilerParams(
             collective_id=0, has_side_effects=True, vmem_limit_bytes=56 * 1024 * 1024

time: 95.5 us -> 93.9 us (0.983)
  Pallas kernels: 92 us -> 90.4 us
    pallas_call x1, Pallas kernels: 92 us -> 90.4 us  [local(): pl.pallas_call(kernel, out_shape=(jax.ShapeDtypeStruct((rows, W), bf16),...]
where the time goes in v3:
time: 93.9 us; the launch traced here: 93.7 us
  Pallas kernels  90.4 us (96%)
  local copies, waits for them, and re-layouts  2.72 us (3%)
    pallas_call x1, Pallas kernels, local(): pl.pallas_call(kernel, out_shape=(jax.ShapeDtypeStruct((rows, W), bf16),...  90.4 us
    unnamed x4, local copies, waits for them, and re-layouts  2.72 us

profile of v3, /device:TPU:1, one launch (start us, length us, event | category | flops | bytes accessed | tf_op | source)
XLA Modules:
  0.0 93.7 jit_solution(12230206043213671693)
XLA Ops:
  0.6 90.4 %lattice.1 = (bf16[2048,128]{1,0:T(8,128)(2,1)}, bf16[2048,128]{1,0:T(8,128)(2,1)}) custom-call(bf16[2048,128]{1,0:T(8,128)(2,1)} %fwd.1, bf16[2048,128]{1,0:T(8,128)(2,1)} %bwd.1), custom_call_target="tpu_custom_call" | custom-call | tf_op jit(solution)/shard_map/lattice/pallas_call | solution.py:504
  91.0 0.0 copy-start
  91.0 1.9 %copy.6 = bf16[2048,128]{1,0:T(8,128)(2,1)} copy(bf16[2048,128]{1,0:T(8,128)(2,1)} %get-tuple-element.4) | data formatting | bytes 1048576
  92.9 0.0 copy-done
  92.9 0.8 copy.7
Async XLA Ops:
  91.0 1.9 %copy-start = (bf16[2048,128]{1,0:T(8,128)(2,1)S(1)}, bf16[2048,128]{1,0:T(8,128)(2,1)}, u32[]{:S(2)}) copy-start(bf16[2048,128]{1,0:T(8,128)(2,1)} %get-tuple-element.5) | copy-start | bytes 1572868
